TPU v7x, 32 devices: a whole 2x2x4 slice. The times are simulated.
32 devices in a mesh: row: 8 (over z, core), col: 4 (over y, x).
Axes of the slice: x: 2, y: 2, z: 4, core: 2. Of those that a mesh axis runs over, the one named last changes fastest.
Arguments:
- right_sides: float32 [4, 1024, 4096], P(None, 'row', 'col'), may hold values from -6 to 6
- low_left: bfloat16 [6, 4096, 128], P(None, 'col'), may hold values from -0.25 to 0.25
- low_right: bfloat16 [6, 4096, 128], P(None, 'col'), may hold values from -0.09375 to 0.09375
- up_left: bfloat16 [6, 4096, 128], P(None, 'col'), may hold values from -0.25 to 0.25
- up_right: bfloat16 [6, 4096, 128], P(None, 'col'), may hold values from -0.09375 to 0.09375
- low_ranks: int32 [6], replicated, may hold values from 1 to 4
- up_ranks: int32 [6], replicated, may hold values from 1 to 4
- inv_lower: bfloat16 [4, 4096, 4096], P(None, 'col', 'row'), may hold values from -0.09375 to 0.09375
- inv_upper: bfloat16 [4, 4096, 4096], P(None, 'col', 'row'), may hold values from -0.09375 to 0.09375
Outputs:
- solution: float32 [4, 1024, 4096], P(None, 'row', 'col')
Inputs may be any that keep to these rules, and one draw needn't show every extreme that they name: `low_ranks`: factor columns beyond 32 times this value are padding with arbitrary values and must be masked out. `up_ranks`: factor columns beyond 32 times this value are padding with arbitrary values and must be masked out.
All inputs are finite; a program needn't handle non-finite values.
Results may differ from a plain program's by a relative error of at most 0.03.
Values may be sent and summed in bfloat16 or wider, within the bound.
A program may use at most 64 MiB of HBM per device.

v0:
```python
import jax
import jax.numpy as jnp
import numpy as np
from jax import lax
from jax.sharding import PartitionSpec as P

RBLK = 32


def rank_mask(ranks, pair_index, rank_cols):
    columns = jnp.arange(rank_cols, dtype=jnp.int32)
    return (columns[None, :] < RBLK * ranks[pair_index][:, None]).astype(jnp.float32)


def times_inverse(block, inverse):
    return lax.dot_general(
        block, inverse, (((1,), (1,)), ((), ())), preferred_element_type=jnp.float32
    )


def sum_terms(moved, inverse):
    return times_inverse(moved, inverse)


def shards(
    right_sides, low_left, low_right, up_left, up_right, low_ranks, up_ranks, inv_lower, inv_upper
):
    tile_count = right_sides.shape[0]
    rank_cols = low_left.shape[2]
    residual = right_sides
    forward = []
    for section in range(tile_count):
        rounded = residual[section].astype(jnp.bfloat16)
        whole = lax.all_gather(rounded, "col", axis=1, tiled=True)
        moved = lax.all_to_all(whole, "row", split_axis=1, concat_axis=0, tiled=True)
        solved = lax.psum_scatter(
            sum_terms(moved, inv_lower[section]).astype(jnp.bfloat16),
            "row",
            scatter_dimension=0,
            tiled=True,
        ).astype(jnp.float32)
        forward.append(solved)
        if section + 1 < tile_count:
            pair_index = np.array(
                [tile * (tile - 1) // 2 + section for tile in range(section + 1, tile_count)],
                dtype=np.int32,
            )
            projections = jnp.einsum(
                "nw,mwr->mnr",
                solved.astype(jnp.bfloat16),
                low_right[pair_index],
                preferred_element_type=jnp.float32,
            )
            leading = lax.psum(projections[:1].astype(jnp.bfloat16), "col").astype(jnp.float32)
            if section + 2 < tile_count:
                remaining = lax.psum(projections[1:].astype(jnp.bfloat16), "col").astype(
                    jnp.float32
                )
                summed = jnp.concatenate([leading, remaining], axis=0)
            else:
                summed = leading
            masked = (summed * rank_mask(low_ranks, pair_index, rank_cols)[:, None, :]).astype(
                jnp.bfloat16
            )
            update = jnp.einsum(
                "mnr,mwr->mnw", masked, low_left[pair_index], preferred_element_type=jnp.float32
            )
            residual = residual.at[section + 1 :].add(-update)
    state = jnp.stack(forward)
    solutions = [None] * tile_count
    for section in range(tile_count - 1, -1, -1):
        rounded = state[section].astype(jnp.bfloat16)
        whole = lax.all_gather(rounded, "col", axis=1, tiled=True)
        moved = lax.all_to_all(whole, "row", split_axis=1, concat_axis=0, tiled=True)
        solved = lax.psum_scatter(
            sum_terms(moved, inv_upper[section]).astype(jnp.bfloat16),
            "row",
            scatter_dimension=0,
            tiled=True,
        ).astype(jnp.float32)
        solutions[section] = solved
        if section > 0:
            pair_index = np.array(
                [section * (section - 1) // 2 + tile for tile in range(section)], dtype=np.int32
            )
            projections = jnp.einsum(
                "nw,mwr->mnr",
                solved.astype(jnp.bfloat16),
                up_right[pair_index],
                preferred_element_type=jnp.float32,
            )
            leading = lax.psum(projections[-1:].astype(jnp.bfloat16), "col").astype(jnp.float32)
            if section > 1:
                remaining = lax.psum(projections[:-1].astype(jnp.bfloat16), "col").astype(
                    jnp.float32
                )
                summed = jnp.concatenate([remaining, leading], axis=0)
            else:
                summed = leading
            masked = (summed * rank_mask(up_ranks, pair_index, rank_cols)[:, None, :]).astype(
                jnp.bfloat16
            )
            update = jnp.einsum(
                "mnr,mwr->mnw", masked, up_left[pair_index], preferred_element_type=jnp.float32
            )
            state = state.at[:section].add(-update)
    return jnp.stack(solutions)


def solution(mesh):
    in_specs = (
        P(None, "row", "col"),
        P(None, "col", None),
        P(None, "col", None),
        P(None, "col", None),
        P(None, "col", None),
        P(),
        P(),
        P(None, "col", "row"),
        P(None, "col", "row"),
    )
    out_specs = P(None, "row", "col")
    return jax.shard_map(shards, mesh=mesh, in_specs=in_specs, out_specs=out_specs, check_vma=False)
```

profile of v0, /device:TPU:0, one launch (start us, length us, event | category | flops | bytes accessed | tf_op | source)
XLA Modules:
  0.0 1013.5 jit_solution(5519528377490401830)
XLA Ops:
  8.5 29.9 %all-gather.18.cloned.1.call-done = bf16[1,128,4096]{1,2,0:T(8,128)(2,1)} async-done(((bf16[1,128,1024]{1,2,0:T(8,128)(2,1)}), bf16[1,128,4096]{1,2,0:T(8,128)(2,1)}) %all-gather.18.cloned.1.call-update) | async-done | bytes 1048592 | tf_op jit(solution)/shard_map/all_gather | solution.py:34
  38.4 31.2 %all_to_all.152 = bf16[128,8,512]{0,2,1:T(8,128)(2,1)S(1)} all-to-all(bf16[128,8,512]{0,2,1:T(8,128)(2,1)} %bitcast.171), channel_id=1, replica_groups=mesh['row'=8,'col'=4] {'row'}, dimensions={1} | all-to-all | bytes 2097152 | tf_op jit(solution)/shard_map/all_to_all | solution.py:35
  70.1 3.8 convolution_convert_fusion.7
  76.8 31.4 %reduce-scatter.9.cloned.1.call-done = bf16[128,1024]{1,0:T(8,128)(2,1)} async-done(((bf16[1024,1024]{1,0:T(8,128)(2,1)}), bf16[128,1024]{1,0:T(8,128)(2,1)}) %reduce-scatter.9.cloned.1.call-update) | async-done | bytes 262160 | tf_op jit(solution)/shard_map/reduce_scatter | solution.py:36
  108.2 1.4 fusion.8
  111.1 16.1 %psum.70 = bf16[1,128,128]{1,2,0:T(8,128)(2,1)S(1)} all-reduce(bf16[1,128,128]{1,2,0:T(8,128)(2,1)S(1)} %slice.332), channel_id=1, replica_groups=mesh['row'=8,'col'=4] {'col'}, use_global_device_ids=true, to_apply=%region_1.0 | all-reduce | flops 16384 | bytes 65536 | tf_op jit(solution)/shard_map/psum | solution.py:54
  127.2 24.3 %all-reduce.7.cloned.1.call-done = bf16[2,128,128]{1,2,0:T(8,128)(2,1)} async-done(((bf16[2,128,128]{1,2,0:T(8,128)(2,1)}), bf16[2,128,128]{1,2,0:T(8,128)(2,1)}) %all-reduce.7.cloned.1.call-update) | async-done | bytes 65552 | tf_op jit(solution)/shard_map/psum | solution.py:56
  151.5 2.0 negate_add_fusion.1
  154.2 26.6 %all-gather.20.cloned.1.call-done = bf16[1,128,4096]{2,1,0:T(8,128)(2,1)} async-done(((bf16[1,128,1024]{2,1,0:T(8,128)(2,1)}), bf16[1,128,4096]{2,1,0:T(8,128)(2,1)}) %all-gather.20.cloned.1.call-update) | async-done | bytes 1048592 | tf_op jit(solution)/shard_map/all_gather | solution.py:34
  180.8 1.6 copy.84
  182.8 31.0 %all_to_all.153 = bf16[128,8,512]{2,0,1:T(8,128)(2,1)S(1)} all-to-all(bf16[128,8,512]{2,0,1:T(8,128)(2,1)S(1)} %copy.61), channel_id=1, replica_groups=mesh['row'=8,'col'=4] {'row'}, dimensions={1} | all-to-all | bytes 2097152 | tf_op jit(solution)/shard_map/all_to_all | solution.py:35
  213.8 3.8 convolution_convert_fusion.6
  218.2 2.1 gather_fusion.3
  220.9 30.8 %reduce-scatter.11.cloned.1.call-done = bf16[128,1024]{1,0:T(8,128)(2,1)} async-done(((bf16[1024,1024]{1,0:T(8,128)(2,1)}), bf16[128,1024]{1,0:T(8,128)(2,1)}) %reduce-scatter.11.cloned.1.call-update) | async-done | bytes 262160 | tf_op jit(solution)/shard_map/reduce_scatter | solution.py:36
  251.8 1.3 fusion.10
  253.9 2.1 gather_fusion.5
  255.9 39.0 %all-reduce.13.cloned.1.call-done = (bf16[1,128,128]{1,2,0:T(8,128)(2,1)}, bf16[1,128,128]{1,2,0:T(8,128)(2,1)}) async-done(((bf16[1,128,128]{1,2,0:T(8,128)(2,1)}, bf16[1,128,128]{1,2,0:T(8,128)(2,1)}), (bf16[1,128,128]{1,2,0:T(8,128)(2,1)}, bf16[1,128,128]{1,2,0:T(8,128)(2,1)})) %all-reduce.13.cloned.1.call-update) | async-done | bytes 65552 | tf_op jit(solution)/shard_map/psum | solution.py:56
  294.9 1.2 fusion
  297.0 26.6 %all-gather.22.cloned.1.call-done = bf16[1,128,4096]{2,1,0:T(8,128)(2,1)} async-done(((bf16[1,128,1024]{2,1,0:T(8,128)(2,1)}), bf16[1,128,4096]{2,1,0:T(8,128)(2,1)}) %all-gather.22.cloned.1.call-update) | async-done | bytes 1048592 | tf_op jit(solution)/shard_map/all_gather | solution.py:34
  323.6 1.6 copy.85
  325.5 31.0 %all_to_all.154 = bf16[128,8,512]{2,0,1:T(8,128)(2,1)S(1)} all-to-all(bf16[128,8,512]{2,0,1:T(8,128)(2,1)S(1)} %copy.64), channel_id=1, replica_groups=mesh['row'=8,'col'=4] {'row'}, dimensions={1} | all-to-all | bytes 2097152 | tf_op jit(solution)/shard_map/all_to_all | solution.py:35
  356.5 3.8 convolution_convert_fusion.5
  361.6 32.9 %reduce-scatter.13.cloned.1.call-done = bf16[128,1024]{1,0:T(8,128)(2,1)} async-done(((bf16[1024,1024]{1,0:T(8,128)(2,1)}), bf16[128,1024]{1,0:T(8,128)(2,1)}) %reduce-scatter.13.cloned.1.call-update) | async-done | bytes 262160 | tf_op jit(solution)/shard_map/reduce_scatter | solution.py:36
  394.5 1.2 fusion.12
  395.8 16.2 %psum.74 = bf16[1,128,128]{2,1,0:T(8,128)(2,1)S(1)} all-reduce(bf16[1,128,128]{2,1,0:T(8,128)(2,1)S(1)} %fusion.12), channel_id=1, replica_groups=mesh['row'=8,'col'=4] {'col'}, use_global_device_ids=true, to_apply=%region_7.0 | all-reduce | flops 16384 | bytes 65536 | tf_op jit(solution)/shard_map/psum | solution.py:54
  412.0 1.9 fusion.7
  414.0 23.0 %all-gather.24.cloned.1.call-done = bf16[1,128,4096]{2,1,0:T(8,128)(2,1)} async-done(((bf16[1,128,1024]{2,1,0:T(8,128)(2,1)}), bf16[1,128,4096]{2,1,0:T(8,128)(2,1)}) %all-gather.24.cloned.1.call-update) | async-done | bytes 1048592 | tf_op jit(solution)/shard_map/all_gather | solution.py:34
  437.0 1.6 copy.86
  438.9 31.0 %all_to_all.155 = bf16[128,8,512]{2,0,1:T(8,128)(2,1)S(1)} all-to-all(bf16[128,8,512]{2,0,1:T(8,128)(2,1)S(1)} %copy.65), channel_id=1, replica_groups=mesh['row'=8,'col'=4] {'row'}, dimensions={1} | all-to-all | bytes 2097152 | tf_op jit(solution)/shard_map/all_to_all | solution.py:35
  469.9 3.8 convolution_convert_fusion.4
  473.8 34.1 %reduce-scatter.15.cloned.1.call-done = bf16[128,1024]{1,0:T(8,128)(2,1)} async-done(((bf16[1024,1024]{1,0:T(8,128)(2,1)}), bf16[128,1024]{1,0:T(8,128)(2,1)}) %reduce-scatter.15.cloned.1.call-update) | async-done | bytes 262160 | tf_op jit(solution)/shard_map/reduce_scatter | solution.py:36
  508.0 26.8 %all-gather.16.cloned.1.call-done = bf16[128,4096]{1,0:T(8,128)(2,1)} async-done(((bf16[128,1024]{1,0:T(8,128)(2,1)}), bf16[128,4096]{1,0:T(8,128)(2,1)}) %all-gather.16.cloned.1.call-update) | async-done | bytes 1048592 | tf_op jit(solution)/shard_map/all_gather | solution.py:73
  534.8 1.3 copy.91
  536.1 31.0 %all_to_all.156 = bf16[128,8,512]{2,0,1:T(8,128)(2,1)S(1)} all-to-all(bf16[128,8,512]{2,0,1:T(8,128)(2,1)S(1)} %bitcast.165), channel_id=1, replica_groups=mesh['row'=8,'col'=4] {'row'}, dimensions={1} | all-to-all | bytes 2097152 | tf_op jit(solution)/shard_map/all_to_all | solution.py:74
  567.1 3.8 convolution_convert_fusion.3
  573.8 31.4 %reduce-scatter.17.cloned.1.call-done = bf16[128,1024]{1,0:T(8,128)(2,1)} async-done(((bf16[1024,1024]{1,0:T(8,128)(2,1)}), bf16[128,1024]{1,0:T(8,128)(2,1)}) %reduce-scatter.17.cloned.1.call-update) | async-done | bytes 262160 | tf_op jit(solution)/shard_map/reduce_scatter | solution.py:75
  605.1 1.4 fusion.9
  608.0 16.3 %psum.76 = bf16[1,128,128]{1,2,0:T(8,128)(2,1)S(1)} all-reduce(bf16[1,128,128]{1,2,0:T(8,128)(2,1)S(1)} %slice.341), channel_id=1, replica_groups=mesh['row'=8,'col'=4] {'col'}, use_global_device_ids=true, to_apply=%region_11.0 | all-reduce | flops 16384 | bytes 65536 | tf_op jit(solution)/shard_map/psum | solution.py:92
  624.3 24.1 %all-reduce.9.cloned.1.call-done = bf16[2,128,128]{1,2,0:T(8,128)(2,1)} async-done(((bf16[2,128,128]{1,2,0:T(8,128)(2,1)}), bf16[2,128,128]{1,2,0:T(8,128)(2,1)}) %all-reduce.9.cloned.1.call-update) | async-done | bytes 65552 | tf_op jit(solution)/shard_map/psum | solution.py:94
  648.4 1.4 negate_add_fusion
  650.6 26.6 %all-gather.26.cloned.1.call-done = bf16[1,128,4096]{2,1,0:T(8,128)(2,1)} async-done(((bf16[1,128,1024]{2,1,0:T(8,128)(2,1)}), bf16[1,128,4096]{2,1,0:T(8,128)(2,1)}) %all-gather.26.cloned.1.call-update) | async-done | bytes 1048592 | tf_op jit(solution)/shard_map/all_gather | solution.py:73
  677.2 1.6 copy.87
  679.1 31.0 %all_to_all.157 = bf16[128,8,512]{2,0,1:T(8,128)(2,1)S(1)} all-to-all(bf16[128,8,512]{2,0,1:T(8,128)(2,1)S(1)} %copy.69), channel_id=1, replica_groups=mesh['row'=8,'col'=4] {'row'}, dimensions={1} | all-to-all | bytes 2097152 | tf_op jit(solution)/shard_map/all_to_all | solution.py:74
  710.1 3.8 convolution_convert_fusion.2
  714.6 2.1 gather_fusion.9
  717.3 30.9 %reduce-scatter.19.cloned.1.call-done = bf16[128,1024]{1,0:T(8,128)(2,1)} async-done(((bf16[1024,1024]{1,0:T(8,128)(2,1)}), bf16[128,1024]{1,0:T(8,128)(2,1)}) %reduce-scatter.19.cloned.1.call-update) | async-done | bytes 262160 | tf_op jit(solution)/shard_map/reduce_scatter | solution.py:75
  748.1 1.3 fusion.11
  750.2 2.1 gather_fusion.11
  752.3 39.0 %all-reduce.11.cloned.1.call-done = (bf16[1,128,128]{1,2,0:T(8,128)(2,1)}, bf16[1,128,128]{1,2,0:T(8,128)(2,1)}) async-done(((bf16[1,128,128]{1,2,0:T(8,128)(2,1)}, bf16[1,128,128]{1,2,0:T(8,128)(2,1)}), (bf16[1,128,128]{1,2,0:T(8,128)(2,1)}, bf16[1,128,128]{1,2,0:T(8,128)(2,1)})) %all-reduce.11.cloned.1.call-update) | async-done | bytes 65552 | tf_op jit(solution)/shard_map/psum | solution.py:92
  791.3 1.2 fusion.1
  793.3 26.6 %all-gather.28.cloned.1.call-done = bf16[1,128,4096]{2,1,0:T(8,128)(2,1)} async-done(((bf16[1,128,1024]{2,1,0:T(8,128)(2,1)}), bf16[1,128,4096]{2,1,0:T(8,128)(2,1)}) %all-gather.28.cloned.1.call-update) | async-done | bytes 1048592 | tf_op jit(solution)/shard_map/all_gather | solution.py:73
  819.9 1.6 copy.88
  821.8 31.0 %all_to_all.158 = bf16[128,8,512]{2,0,1:T(8,128)(2,1)S(1)} all-to-all(bf16[128,8,512]{2,0,1:T(8,128)(2,1)S(1)} %copy.72), channel_id=1, replica_groups=mesh['row'=8,'col'=4] {'row'}, dimensions={1} | all-to-all | bytes 2097152 | tf_op jit(solution)/shard_map/all_to_all | solution.py:74
  852.8 3.8 convolution_convert_fusion.1
  856.7 34.1 %reduce-scatter.21.cloned.1.call-done = bf16[128,1024]{1,0:T(8,128)(2,1)} async-done(((bf16[1024,1024]{1,0:T(8,128)(2,1)}), bf16[128,1024]{1,0:T(8,128)(2,1)}) %reduce-scatter.21.cloned.1.call-update) | async-done | bytes 262160 | tf_op jit(solution)/shard_map/reduce_scatter | solution.py:75
  890.8 1.2 fusion.13
  892.0 16.2 %psum.79 = bf16[1,128,128]{2,1,0:T(8,128)(2,1)S(1)} all-reduce(bf16[1,128,128]{2,1,0:T(8,128)(2,1)S(1)} %fusion.13), channel_id=1, replica_groups=mesh['row'=8,'col'=4] {'col'}, use_global_device_ids=true, to_apply=%region_16.0 | all-reduce | flops 16384 | bytes 65536 | tf_op jit(solution)/shard_map/psum | solution.py:92
  908.2 1.9 fusion.6
  910.2 23.0 %all-gather.30.cloned.1.call-done = bf16[1,128,4096]{2,1,0:T(8,128)(2,1)} async-done(((bf16[1,128,1024]{2,1,0:T(8,128)(2,1)}), bf16[1,128,4096]{2,1,0:T(8,128)(2,1)}) %all-gather.30.cloned.1.call-update) | async-done | bytes 1048592 | tf_op jit(solution)/shard_map/all_gather | solution.py:73
  933.2 1.6 copy.89
  935.1 31.0 %all_to_all.159 = bf16[128,8,512]{2,0,1:T(8,128)(2,1)S(1)} all-to-all(bf16[128,8,512]{2,0,1:T(8,128)(2,1)S(1)} %copy.73), channel_id=1, replica_groups=mesh['row'=8,'col'=4] {'row'}, dimensions={1} | all-to-all | bytes 2097152 | tf_op jit(solution)/shard_map/all_to_all | solution.py:74
  966.1 3.8 convolution_convert_fusion
  970.0 34.2 %reduce-scatter.23.cloned.1.call-done = bf16[128,1024]{1,0:T(8,128)(2,1)} async-done(((bf16[1024,1024]{1,0:T(8,128)(2,1)}), bf16[128,1024]{1,0:T(8,128)(2,1)}) %reduce-scatter.23.cloned.1.call-update) | async-done | bytes 262160 | tf_op jit(solution)/shard_map/reduce_scatter | solution.py:75
  1004.2 2.4 maximum_convert_fusion
  (114 shorter events, 21.1 us)
Async XLA Ops:
  6.5 31.9 %all-gather.18.cloned.1.call-start = ((), (), s32[]{:S(2)}) async-start(), calls=%async_computation.27 | async-start | bytes 1310720 | tf_op jit(solution)/shard_map/all_gather | solution.py:34
  8.5 99.7 %reduce-scatter.9.cloned.1.call-start = ((), (), s32[]{:S(2)}) async-start(), calls=%async_computation.16 | async-start | bytes 2359296 | tf_op jit(solution)/shard_map/reduce_scatter | solution.py:36
  74.0 0.7 copy-start.15
  74.0 1.4 copy-start.2
  74.0 2.1 copy-start
  74.0 77.5 %all-reduce.7.cloned.1.call-start = ((), (), s32[]{:S(2)}) async-start(), calls=%async_computation.17 | async-start | bytes 131072 | tf_op jit(solution)/shard_map/psum | solution.py:56
  76.1 34.2 %copy-start.4 = (bf16[6,1024,128]{2,1,0:T(8,128)(2,1)S(1)}, bf16[6,1024,128]{2,1,0:T(8,128)(2,1)}, u32[]{:S(2)}) copy-start(bf16[6,1024,128]{2,1,0:T(8,128)(2,1)} %param.46) | copy-start | bytes 4718596
  110.2 70.6 %all-gather.20.cloned.1.call-start = ((), (), s32[]{:S(2)}) async-start(), calls=%async_computation.28 | async-start | bytes 1310720 | tf_op jit(solution)/shard_map/all_gather | solution.py:34
  154.2 97.6 %reduce-scatter.11.cloned.1.call-start = ((), (), s32[]{:S(2)}) async-start(), calls=%async_computation.18 | async-start | bytes 2359296 | tf_op jit(solution)/shard_map/reduce_scatter | solution.py:36
  217.6 0.7 copy-start.14
  217.6 77.3 %all-reduce.13.cloned.1.call-start = ((), (), s32[]{:S(2)}) async-start(), calls=%async_computation.35 | async-start | bytes 131072 | tf_op jit(solution)/shard_map/psum | solution.py:56
  253.7 69.8 %all-gather.22.cloned.1.call-start = ((), (), s32[]{:S(2)}) async-start(), calls=%async_computation.29 | async-start | bytes 1310720 | tf_op jit(solution)/shard_map/all_gather | solution.py:34
  296.9 97.6 %reduce-scatter.13.cloned.1.call-start = ((), (), s32[]{:S(2)}) async-start(), calls=%async_computation.19 | async-start | bytes 2359296 | tf_op jit(solution)/shard_map/reduce_scatter | solution.py:36
  360.3 76.7 %all-gather.24.cloned.1.call-start = ((), (), s32[]{:S(2)}) async-start(), calls=%async_computation.30 | async-start | bytes 1310720 | tf_op jit(solution)/shard_map/all_gather | solution.py:34
  413.9 94.0 %reduce-scatter.15.cloned.1.call-start = ((), (), s32[]{:S(2)}) async-start(), calls=%async_computation.20 | async-start | bytes 2359296 | tf_op jit(solution)/shard_map/reduce_scatter | solution.py:36
  473.8 61.0 %all-gather.16.cloned.1.call-start = ((), (), s32[]{:S(2)}) async-start(), calls=%async_computation.21 | async-start | bytes 1310720 | tf_op jit(solution)/shard_map/all_gather | solution.py:73
  508.0 97.2 %reduce-scatter.17.cloned.1.call-start = ((), (), s32[]{:S(2)}) async-start(), calls=%async_computation.22 | async-start | bytes 2359296 | tf_op jit(solution)/shard_map/reduce_scatter | solution.py:75
  570.9 0.7 copy-start.13
  570.9 1.4 copy-start.3
  570.9 2.1 copy-start.1
  571.0 77.4 %all-reduce.9.cloned.1.call-start = ((), (), s32[]{:S(2)}) async-start(), calls=%async_computation.23 | async-start | bytes 131072 | tf_op jit(solution)/shard_map/psum | solution.py:94
  573.1 34.2 %copy-start.5 = (bf16[6,1024,128]{2,1,0:T(8,128)(2,1)S(1)}, bf16[6,1024,128]{2,1,0:T(8,128)(2,1)}, u32[]{:S(2)}) copy-start(bf16[6,1024,128]{2,1,0:T(8,128)(2,1)} %param.48) | copy-start | bytes 4718596
  573.1 75.3 %copy-start.9 = (bf16[128,1024]{1,0:T(8,128)(2,1)S(1)}, bf16[128,1024]{1,0:T(8,128)(2,1)}, u32[]{:S(2)}) copy-start(bf16[128,1024]{1,0:T(8,128)(2,1)} %reduce-scatter.11.cloned.1.call-done) | copy-start | bytes 786436
  573.1 75.3 %copy-start.10 = (bf16[128,1024]{1,0:T(8,128)(2,1)S(1)}, bf16[128,1024]{1,0:T(8,128)(2,1)}, u32[]{:S(2)}) copy-start(bf16[128,1024]{1,0:T(8,128)(2,1)} %reduce-scatter.13.cloned.1.call-done) | copy-start | bytes 786436
  573.1 75.3 %copy-start.11 = (bf16[128,1024]{1,0:T(8,128)(2,1)S(1)}, bf16[128,1024]{1,0:T(8,128)(2,1)}, u32[]{:S(2)}) copy-start(bf16[128,1024]{1,0:T(8,128)(2,1)} %reduce-scatter.9.cloned.1.call-done) | copy-start | bytes 786436
  607.2 70.0 %all-gather.26.cloned.1.call-start = ((), (), s32[]{:S(2)}) async-start(), calls=%async_computation.31 | async-start | bytes 1310720 | tf_op jit(solution)/shard_map/all_gather | solution.py:73
  650.5 97.6 %reduce-scatter.19.cloned.1.call-start = ((), (), s32[]{:S(2)}) async-start(), calls=%async_computation.24 | async-start | bytes 2359296 | tf_op jit(solution)/shard_map/reduce_scatter | solution.py:75
  713.9 0.7 copy-start.12
  713.9 77.3 %all-reduce.11.cloned.1.call-start = ((), (), s32[]{:S(2)}) async-start(), calls=%async_computation.34 | async-start | bytes 131072 | tf_op jit(solution)/shard_map/psum | solution.py:92
  750.1 69.8 %all-gather.28.cloned.1.call-start = ((), (), s32[]{:S(2)}) async-start(), calls=%async_computation.32 | async-start | bytes 1310720 | tf_op jit(solution)/shard_map/all_gather | solution.py:73
  793.2 97.6 %reduce-scatter.21.cloned.1.call-start = ((), (), s32[]{:S(2)}) async-start(), calls=%async_computation.25 | async-start | bytes 2359296 | tf_op jit(solution)/shard_map/reduce_scatter | solution.py:75
  856.6 76.6 %all-gather.30.cloned.1.call-start = ((), (), s32[]{:S(2)}) async-start(), calls=%async_computation.33 | async-start | bytes 1310720 | tf_op jit(solution)/shard_map/all_gather | solution.py:73
  910.1 94.0 %reduce-scatter.23.cloned.1.call-start = ((), (), s32[]{:S(2)}) async-start(), calls=%async_computation.26 | async-start | bytes 2359296 | tf_op jit(solution)/shard_map/reduce_scatter | solution.py:75
  969.9 34.2 %copy-start.6 = (bf16[128,1024]{1,0:T(8,128)(2,1)S(1)}, bf16[128,1024]{1,0:T(8,128)(2,1)}, u32[]{:S(2)}) copy-start(bf16[128,1024]{1,0:T(8,128)(2,1)} %reduce-scatter.19.cloned.1.call-done) | copy-start | bytes 786436
  969.9 34.2 %copy-start.7 = (bf16[128,1024]{1,0:T(8,128)(2,1)S(1)}, bf16[128,1024]{1,0:T(8,128)(2,1)}, u32[]{:S(2)}) copy-start(bf16[128,1024]{1,0:T(8,128)(2,1)} %reduce-scatter.21.cloned.1.call-done) | copy-start | bytes 786436
  969.9 34.2 %copy-start.8 = (bf16[128,1024]{1,0:T(8,128)(2,1)S(1)}, bf16[128,1024]{1,0:T(8,128)(2,1)}, u32[]{:S(2)}) copy-start(bf16[128,1024]{1,0:T(8,128)(2,1)} %reduce-scatter.17.cloned.1.call-done) | copy-start | bytes 786436
Sparse Core Ops, SparseCore 0:
  9.2 29.2 all-gather.17
  74.1 34.0 reduce-scatter.8
  111.1 40.3 all-reduce.6
  154.3 26.4 all-gather.19
  217.7 34.0 reduce-scatter.10
  254.5 40.4 all-reduce.12
  297.0 26.4 all-gather.21
  360.4 34.0 reduce-scatter.12
  414.1 22.9 all-gather.23
  473.9 34.0 reduce-scatter.14
  509.8 24.9 all-gather.15
  571.1 34.0 reduce-scatter.16
  608.0 40.3 all-reduce.8
  650.7 26.4 all-gather.25
  714.1 34.0 reduce-scatter.18
  750.8 40.3 all-reduce.10
  793.3 26.4 all-gather.27
  856.8 34.0 reduce-scatter.20
  910.3 22.8 all-gather.29
  970.1 34.0 reduce-scatter.22
where the time goes:
time: 1020 us; the launch traced here: 1010 us
  waiting for transfers between devices  596 us (58%)
  blocking collectives  313 us (31%)
  matrix products  47.9 us (5%)
  local copies, waits for them, and re-layouts  38.9 us (4%)
  between operations  14.7 us (1%)
    all_to_all x8, blocking collectives, shards(): lax.all_to_all(whole, 'row', split_axis=1, concat_axis=0, tiled=True)  248 us
    all_gather x8, waiting for transfers between devices, shards(): whole = lax.all_gather(rounded, 'col', axis=1, tiled=True)  209 us
    reduce_scatter x4, waiting for transfers between devices, shards(): lax.psum_scatter(sum_terms(moved, inv_upper[section]).astype(jnp.bfloat16...  130 us
    reduce_scatter x4, waiting for transfers between devices, shards(): lax.psum_scatter(sum_terms(moved, inv_lower[section]).astype(jnp.bfloat16...  129 us
    psum x2, waiting for transfers between devices, shards(): lax.psum(projections[1:].astype(jnp.bfloat16), 'col').astype(jnp.float32)  63.3 us
    psum x1, waiting for transfers between devices, shards(): lax.psum(projections[-1:].astype(jnp.bfloat16), 'col').astype(jnp.float32)  39 us
    psum x2, blocking collectives, shards(): lax.psum(projections[-1:].astype(jnp.bfloat16), 'col').astype(jnp.float32)  32.5 us
    psum x2, blocking collectives, shards(): lax.psum(projections[:1].astype(jnp.bfloat16), 'col').astype(jnp.float32)  32.4 us
  transfers between devices with their start and end apart: 20, of which 20 were waited for; matrix products, arithmetic and copies ran while one was open for 1% of the time, Pallas kernels for 0%

commit v1 on v0

--- a/solution.py
+++ b/solution.py
@@ -5,6 +5,7 @@
 from jax.sharding import PartitionSpec as P
 
 RBLK = 32
+slabs_form = lambda tile_in: jnp.sum(lax.all_gather(tile_in, "col"), 0)
 
 
 def rank_mask(ranks, pair_index, rank_cols):
@@ -89,7 +90,7 @@
                 up_right[pair_index],
                 preferred_element_type=jnp.float32,
             )
-            leading = lax.psum(projections[-1:].astype(jnp.bfloat16), "col").astype(jnp.float32)
+            leading = slabs_form(projections[-1:].astype(jnp.bfloat16)).astype(jnp.float32)
             if section > 1:
                 remaining = lax.psum(projections[:-1].astype(jnp.bfloat16), "col").astype(
                     jnp.float32

time: 1020 us -> 987 us (0.968)
  waiting for transfers between devices: 596 us -> 560 us
    psum x1 -> x0, waiting for transfers between devices: 39 us -> none  [shards(): lax.psum(projections[-1:].astype(jnp.bfloat16), 'col').astype(jnp.float32)]
    all_gather x0 -> x3, blocking collectives: none -> 25.6 us  [slabs_form = lambda tile_in: jnp.sum(lax.all_gather(tile_in, 'col'), 0)]
    psum x2 -> x1, blocking collectives: 32.5 us -> 15.3 us  [shards(): lax.psum(projections[:-1].astype(jnp.bfloat16), 'col').astype(jnp.float32)]
  transfers between devices with their start and end apart: 20 -> 19, of which waited for: 20 -> 19; matrix products, arithmetic and copies ran while one was open for 1% -> 2% of each run, Pallas kernels for 0% -> 0%
where the time goes in v1:
time: 987 us; the launch traced here: 985 us
  waiting for transfers between devices  560 us (57%)
  blocking collectives  321 us (33%)
  matrix products  47.2 us (5%)
  local copies, waits for them, and re-layouts  38.8 us (4%)
  between operations  14.4 us (1%)
    all_to_all x8, blocking collectives, shards(): lax.all_to_all(whole, 'row', split_axis=1, concat_axis=0, tiled=True)  248 us
    all_gather x8, waiting for transfers between devices, shards(): whole = lax.all_gather(rounded, 'col', axis=1, tiled=True)  207 us
    reduce_scatter x4, waiting for transfers between devices, shards(): lax.psum_scatter(sum_terms(moved, inv_lower[section]).astype(jnp.bfloat16...  129 us
    reduce_scatter x4, waiting for transfers between devices, shards(): lax.psum_scatter(sum_terms(moved, inv_upper[section]).astype(jnp.bfloat16...  128 us
    psum x2, waiting for transfers between devices, shards(): lax.psum(projections[1:].astype(jnp.bfloat16), 'col').astype(jnp.float32)  63.3 us
    psum x2, blocking collectives, shards(): lax.psum(projections[:1].astype(jnp.bfloat16), 'col').astype(jnp.float32)  32.4 us
    psum x1, waiting for transfers between devices, shards(): lax.psum(projections[:-1].astype(jnp.bfloat16), 'col').astype(jnp.float32)  31.6 us
    dot_general x8, matrix products, times_inverse(): lax.dot_general(block, inverse, (((1,), (1,)), ((), ())), preferred_eleme...  30.6 us
  transfers between devices with their start and end apart: 19, of which 19 were waited for; matrix products, arithmetic and copies ran while one was open for 2% of the time, Pallas kernels for 0%

profile of v1, /device:TPU:0, one launch (start us, length us, event | category | flops | bytes accessed | tf_op | source)
XLA Modules:
  0.0 985.0 jit_solution(2384068761201279928)
XLA Ops:
  8.5 29.9 %all-gather.21.cloned.1.call-done = bf16[1,128,4096]{1,2,0:T(8,128)(2,1)} async-done(((bf16[1,128,1024]{1,2,0:T(8,128)(2,1)}), bf16[1,128,4096]{1,2,0:T(8,128)(2,1)}) %all-gather.21.cloned.1.call-update) | async-done | bytes 1048592 | tf_op jit(solution)/shard_map/all_gather | solution.py:35
  38.4 31.2 %all_to_all.152 = bf16[128,8,512]{0,2,1:T(8,128)(2,1)S(1)} all-to-all(bf16[128,8,512]{0,2,1:T(8,128)(2,1)} %bitcast.170), channel_id=1, replica_groups=mesh['row'=8,'col'=4] {'row'}, dimensions={1} | all-to-all | bytes 2097152 | tf_op jit(solution)/shard_map/all_to_all | solution.py:36
  70.1 3.8 convolution_convert_fusion.7
  76.8 31.4 %reduce-scatter.9.cloned.1.call-done = bf16[128,1024]{1,0:T(8,128)(2,1)} async-done(((bf16[1024,1024]{1,0:T(8,128)(2,1)}), bf16[128,1024]{1,0:T(8,128)(2,1)}) %reduce-scatter.9.cloned.1.call-update) | async-done | bytes 262160 | tf_op jit(solution)/shard_map/reduce_scatter | solution.py:37
  108.2 1.4 fusion.8
  111.1 16.1 %psum.49 = bf16[1,128,128]{1,2,0:T(8,128)(2,1)S(1)} all-reduce(bf16[1,128,128]{1,2,0:T(8,128)(2,1)S(1)} %slice.332), channel_id=1, replica_groups=mesh['row'=8,'col'=4] {'col'}, use_global_device_ids=true, to_apply=%region_1.0 | all-reduce | flops 16384 | bytes 65536 | tf_op jit(solution)/shard_map/psum | solution.py:55
  127.2 24.3 %all-reduce.5.cloned.1.call-done = bf16[2,128,128]{1,2,0:T(8,128)(2,1)} async-done(((bf16[2,128,128]{1,2,0:T(8,128)(2,1)}), bf16[2,128,128]{1,2,0:T(8,128)(2,1)}) %all-reduce.5.cloned.1.call-update) | async-done | bytes 65552 | tf_op jit(solution)/shard_map/psum | solution.py:57
  151.5 2.0 negate_add_fusion.1
  154.2 26.6 %all-gather.23.cloned.1.call-done = bf16[1,128,4096]{2,1,0:T(8,128)(2,1)} async-done(((bf16[1,128,1024]{2,1,0:T(8,128)(2,1)}), bf16[1,128,4096]{2,1,0:T(8,128)(2,1)}) %all-gather.23.cloned.1.call-update) | async-done | bytes 1048592 | tf_op jit(solution)/shard_map/all_gather | solution.py:35
  180.8 1.6 copy.124
  182.8 31.0 %all_to_all.153 = bf16[128,8,512]{2,0,1:T(8,128)(2,1)S(1)} all-to-all(bf16[128,8,512]{2,0,1:T(8,128)(2,1)S(1)} %copy.97), channel_id=1, replica_groups=mesh['row'=8,'col'=4] {'row'}, dimensions={1} | all-to-all | bytes 2097152 | tf_op jit(solution)/shard_map/all_to_all | solution.py:36
  213.8 3.8 convolution_convert_fusion.6
  218.2 2.1 gather_fusion.3
  220.9 30.8 %reduce-scatter.11.cloned.1.call-done = bf16[128,1024]{1,0:T(8,128)(2,1)} async-done(((bf16[1024,1024]{1,0:T(8,128)(2,1)}), bf16[128,1024]{1,0:T(8,128)(2,1)}) %reduce-scatter.11.cloned.1.call-update) | async-done | bytes 262160 | tf_op jit(solution)/shard_map/reduce_scatter | solution.py:37
  251.8 1.3 fusion.10
  253.9 2.1 gather_fusion.5
  255.9 39.0 %all-reduce.9.cloned.1.call-done = (bf16[1,128,128]{1,2,0:T(8,128)(2,1)}, bf16[1,128,128]{1,2,0:T(8,128)(2,1)}) async-done(((bf16[1,128,128]{1,2,0:T(8,128)(2,1)}, bf16[1,128,128]{1,2,0:T(8,128)(2,1)}), (bf16[1,128,128]{1,2,0:T(8,128)(2,1)}, bf16[1,128,128]{1,2,0:T(8,128)(2,1)})) %all-reduce.9.cloned.1.call-update) | async-done | bytes 65552 | tf_op jit(solution)/shard_map/psum | solution.py:57
  294.9 1.2 fusion
  297.0 26.6 %all-gather.25.cloned.1.call-done = bf16[1,128,4096]{2,1,0:T(8,128)(2,1)} async-done(((bf16[1,128,1024]{2,1,0:T(8,128)(2,1)}), bf16[1,128,4096]{2,1,0:T(8,128)(2,1)}) %all-gather.25.cloned.1.call-update) | async-done | bytes 1048592 | tf_op jit(solution)/shard_map/all_gather | solution.py:35
  323.6 1.6 copy.125
  325.5 31.0 %all_to_all.154 = bf16[128,8,512]{2,0,1:T(8,128)(2,1)S(1)} all-to-all(bf16[128,8,512]{2,0,1:T(8,128)(2,1)S(1)} %copy.100), channel_id=1, replica_groups=mesh['row'=8,'col'=4] {'row'}, dimensions={1} | all-to-all | bytes 2097152 | tf_op jit(solution)/shard_map/all_to_all | solution.py:36
  356.5 3.8 convolution_convert_fusion.5
  361.7 32.8 %reduce-scatter.13.cloned.1.call-done = bf16[128,1024]{1,0:T(8,128)(2,1)} async-done(((bf16[1024,1024]{1,0:T(8,128)(2,1)}), bf16[128,1024]{1,0:T(8,128)(2,1)}) %reduce-scatter.13.cloned.1.call-update) | async-done | bytes 262160 | tf_op jit(solution)/shard_map/reduce_scatter | solution.py:37
  394.5 1.2 fusion.12
  395.8 16.2 %psum.53 = bf16[1,128,128]{2,1,0:T(8,128)(2,1)S(1)} all-reduce(bf16[1,128,128]{2,1,0:T(8,128)(2,1)S(1)} %fusion.12), channel_id=1, replica_groups=mesh['row'=8,'col'=4] {'col'}, use_global_device_ids=true, to_apply=%region_7.0 | all-reduce | flops 16384 | bytes 65536 | tf_op jit(solution)/shard_map/psum | solution.py:55
  412.0 1.9 fusion.7
  414.0 23.0 %all-gather.27.cloned.1.call-done = bf16[1,128,4096]{2,1,0:T(8,128)(2,1)} async-done(((bf16[1,128,1024]{2,1,0:T(8,128)(2,1)}), bf16[1,128,4096]{2,1,0:T(8,128)(2,1)}) %all-gather.27.cloned.1.call-update) | async-done | bytes 1048592 | tf_op jit(solution)/shard_map/all_gather | solution.py:35
  437.0 1.6 copy.126
  438.9 31.0 %all_to_all.155 = bf16[128,8,512]{2,0,1:T(8,128)(2,1)S(1)} all-to-all(bf16[128,8,512]{2,0,1:T(8,128)(2,1)S(1)} %copy.101), channel_id=1, replica_groups=mesh['row'=8,'col'=4] {'row'}, dimensions={1} | all-to-all | bytes 2097152 | tf_op jit(solution)/shard_map/all_to_all | solution.py:36
  469.9 3.8 convolution_convert_fusion.4
  473.8 34.1 %reduce-scatter.15.cloned.1.call-done = bf16[128,1024]{1,0:T(8,128)(2,1)} async-done(((bf16[1024,1024]{1,0:T(8,128)(2,1)}), bf16[128,1024]{1,0:T(8,128)(2,1)}) %reduce-scatter.15.cloned.1.call-update) | async-done | bytes 262160 | tf_op jit(solution)/shard_map/reduce_scatter | solution.py:37
  508.0 26.8 %all-gather.19.cloned.1.call-done = bf16[128,4096]{1,0:T(8,128)(2,1)} async-done(((bf16[128,1024]{1,0:T(8,128)(2,1)}), bf16[128,4096]{1,0:T(8,128)(2,1)}) %all-gather.19.cloned.1.call-update) | async-done | bytes 1048592 | tf_op jit(solution)/shard_map/all_gather | solution.py:74
  534.8 1.3 copy.131
  536.1 31.0 %all_to_all.156 = bf16[128,8,512]{2,0,1:T(8,128)(2,1)S(1)} all-to-all(bf16[128,8,512]{2,0,1:T(8,128)(2,1)S(1)} %bitcast.164), channel_id=1, replica_groups=mesh['row'=8,'col'=4] {'row'}, dimensions={1} | all-to-all | bytes 2097152 | tf_op jit(solution)/shard_map/all_to_all | solution.py:75
  567.1 3.8 convolution_convert_fusion.3
  573.8 31.4 %reduce-scatter.17.cloned.1.call-done = bf16[128,1024]{1,0:T(8,128)(2,1)} async-done(((bf16[1024,1024]{1,0:T(8,128)(2,1)}), bf16[128,1024]{1,0:T(8,128)(2,1)}) %reduce-scatter.17.cloned.1.call-update) | async-done | bytes 262160 | tf_op jit(solution)/shard_map/reduce_scatter | solution.py:76
  605.1 1.4 fusion.9
  608.1 8.5 all-gather.4
  616.8 31.6 %all-reduce.7.cloned.1.call-done = bf16[2,128,128]{1,2,0:T(8,128)(2,1)} async-done(((bf16[2,128,128]{1,2,0:T(8,128)(2,1)}), bf16[2,128,128]{1,2,0:T(8,128)(2,1)}) %all-reduce.7.cloned.1.call-update) | async-done | bytes 65552 | tf_op jit(solution)/shard_map/psum | solution.py:95
  648.4 1.4 negate_add_fusion
  650.6 26.6 %all-gather.29.cloned.1.call-done = bf16[1,128,4096]{2,1,0:T(8,128)(2,1)} async-done(((bf16[1,128,1024]{2,1,0:T(8,128)(2,1)}), bf16[1,128,4096]{2,1,0:T(8,128)(2,1)}) %all-gather.29.cloned.1.call-update) | async-done | bytes 1048592 | tf_op jit(solution)/shard_map/all_gather | solution.py:74
  677.2 1.6 copy.127
  679.1 31.0 %all_to_all.157 = bf16[128,8,512]{2,0,1:T(8,128)(2,1)S(1)} all-to-all(bf16[128,8,512]{2,0,1:T(8,128)(2,1)S(1)} %copy.107), channel_id=1, replica_groups=mesh['row'=8,'col'=4] {'row'}, dimensions={1} | all-to-all | bytes 2097152 | tf_op jit(solution)/shard_map/all_to_all | solution.py:75
  710.1 3.8 convolution_convert_fusion.2
  714.6 2.1 gather_fusion.9
  716.6 2.1 gather_fusion.11
  719.5 28.8 %reduce-scatter.19.cloned.1.call-done = bf16[128,1024]{1,0:T(8,128)(2,1)} async-done(((bf16[1024,1024]{1,0:T(8,128)(2,1)}), bf16[128,1024]{1,0:T(8,128)(2,1)}) %reduce-scatter.19.cloned.1.call-update) | async-done | bytes 262160 | tf_op jit(solution)/shard_map/reduce_scatter | solution.py:76
  748.2 1.3 fusion.11
  749.7 8.6 all-gather.6
  758.4 15.3 %psum.55 = bf16[1,128,128]{1,2,0:T(8,128)(2,1)S(1)} all-reduce(bf16[1,128,128]{1,2,0:T(8,128)(2,1)S(1)} %get-tuple-element.145), channel_id=1, replica_groups=mesh['row'=8,'col'=4] {'col'}, use_global_device_ids=true, to_apply=%region_13.0 | all-reduce | flops 16384 | bytes 65536 | tf_op jit(solution)/shard_map/psum | solution.py:95
  775.0 23.5 %all-gather.31.cloned.1.call-done = bf16[1,128,4096]{2,1,0:T(8,128)(2,1)} async-done(((bf16[1,128,1024]{2,1,0:T(8,128)(2,1)}), bf16[1,128,4096]{2,1,0:T(8,128)(2,1)}) %all-gather.31.cloned.1.call-update) | async-done | bytes 1048592 | tf_op jit(solution)/shard_map/all_gather | solution.py:74
  798.5 1.6 copy.128
  800.4 31.0 %all_to_all.158 = bf16[128,8,512]{2,0,1:T(8,128)(2,1)S(1)} all-to-all(bf16[128,8,512]{2,0,1:T(8,128)(2,1)S(1)} %copy.112), channel_id=1, replica_groups=mesh['row'=8,'col'=4] {'row'}, dimensions={1} | all-to-all | bytes 2097152 | tf_op jit(solution)/shard_map/all_to_all | solution.py:75
  831.4 3.8 convolution_convert_fusion.1
  835.3 34.1 %reduce-scatter.21.cloned.1.call-done = bf16[128,1024]{1,0:T(8,128)(2,1)} async-done(((bf16[1024,1024]{1,0:T(8,128)(2,1)}), bf16[128,1024]{1,0:T(8,128)(2,1)}) %reduce-scatter.21.cloned.1.call-update) | async-done | bytes 262160 | tf_op jit(solution)/shard_map/reduce_scatter | solution.py:76
  869.4 1.2 fusion.13
  870.7 8.4 all-gather.8
  879.1 1.9 fusion.6
  881.1 23.9 %all-gather.33.cloned.1.call-done = bf16[1,128,4096]{2,1,0:T(8,128)(2,1)} async-done(((bf16[1,128,1024]{2,1,0:T(8,128)(2,1)}), bf16[1,128,4096]{2,1,0:T(8,128)(2,1)}) %all-gather.33.cloned.1.call-update) | async-done | bytes 1048592 | tf_op jit(solution)/shard_map/all_gather | solution.py:74
  905.0 1.6 copy.129
  907.0 31.0 %all_to_all.159 = bf16[128,8,512]{2,0,1:T(8,128)(2,1)S(1)} all-to-all(bf16[128,8,512]{2,0,1:T(8,128)(2,1)S(1)} %copy.113), channel_id=1, replica_groups=mesh['row'=8,'col'=4] {'row'}, dimensions={1} | all-to-all | bytes 2097152 | tf_op jit(solution)/shard_map/all_to_all | solution.py:75
  937.9 3.8 convolution_convert_fusion
  941.8 34.2 %reduce-scatter.23.cloned.1.call-done = bf16[128,1024]{1,0:T(8,128)(2,1)} async-done(((bf16[1024,1024]{1,0:T(8,128)(2,1)}), bf16[128,1024]{1,0:T(8,128)(2,1)}) %reduce-scatter.23.cloned.1.call-update) | async-done | bytes 262160 | tf_op jit(solution)/shard_map/reduce_scatter | solution.py:76
  976.0 2.4 maximum_convert_fusion
  (120 shorter events, 21.4 us)
Async XLA Ops:
  6.5 31.9 %all-gather.21.cloned.1.call-start = ((), (), s32[]{:S(2)}) async-start(), calls=%async_computation.27 | async-start | bytes 1310720 | tf_op jit(solution)/shard_map/all_gather | solution.py:35
  8.5 99.7 %reduce-scatter.9.cloned.1.call-start = ((), (), s32[]{:S(2)}) async-start(), calls=%async_computation.16 | async-start | bytes 2359296 | tf_op jit(solution)/shard_map/reduce_scatter | solution.py:37
  74.0 0.7 copy-start.15
  74.0 1.4 copy-start.2
  74.0 2.1 copy-start
  74.0 77.5 %all-reduce.5.cloned.1.call-start = ((), (), s32[]{:S(2)}) async-start(), calls=%async_computation.17 | async-start | bytes 131072 | tf_op jit(solution)/shard_map/psum | solution.py:57
  76.1 34.2 %copy-start.4 = (bf16[6,1024,128]{2,1,0:T(8,128)(2,1)S(1)}, bf16[6,1024,128]{2,1,0:T(8,128)(2,1)}, u32[]{:S(2)}) copy-start(bf16[6,1024,128]{2,1,0:T(8,128)(2,1)} %param.46) | copy-start | bytes 4718596
  110.2 70.6 %all-gather.23.cloned.1.call-start = ((), (), s32[]{:S(2)}) async-start(), calls=%async_computation.28 | async-start | bytes 1310720 | tf_op jit(solution)/shard_map/all_gather | solution.py:35
  154.2 97.6 %reduce-scatter.11.cloned.1.call-start = ((), (), s32[]{:S(2)}) async-start(), calls=%async_computation.18 | async-start | bytes 2359296 | tf_op jit(solution)/shard_map/reduce_scatter | solution.py:37
  217.6 0.7 copy-start.14
  217.6 77.3 %all-reduce.9.cloned.1.call-start = ((), (), s32[]{:S(2)}) async-start(), calls=%async_computation.34 | async-start | bytes 131072 | tf_op jit(solution)/shard_map/psum | solution.py:57
  253.7 69.8 %all-gather.25.cloned.1.call-start = ((), (), s32[]{:S(2)}) async-start(), calls=%async_computation.29 | async-start | bytes 1310720 | tf_op jit(solution)/shard_map/all_gather | solution.py:35
  296.9 97.6 %reduce-scatter.13.cloned.1.call-start = ((), (), s32[]{:S(2)}) async-start(), calls=%async_computation.19 | async-start | bytes 2359296 | tf_op jit(solution)/shard_map/reduce_scatter | solution.py:37
  360.3 76.7 %all-gather.27.cloned.1.call-start = ((), (), s32[]{:S(2)}) async-start(), calls=%async_computation.30 | async-start | bytes 1310720 | tf_op jit(solution)/shard_map/all_gather | solution.py:35
  413.9 94.0 %reduce-scatter.15.cloned.1.call-start = ((), (), s32[]{:S(2)}) async-start(), calls=%async_computation.20 | async-start | bytes 2359296 | tf_op jit(solution)/shard_map/reduce_scatter | solution.py:37
  473.8 61.0 %all-gather.19.cloned.1.call-start = ((), (), s32[]{:S(2)}) async-start(), calls=%async_computation.21 | async-start | bytes 1310720 | tf_op jit(solution)/shard_map/all_gather | solution.py:74
  508.0 97.2 %reduce-scatter.17.cloned.1.call-start = ((), (), s32[]{:S(2)}) async-start(), calls=%async_computation.22 | async-start | bytes 2359296 | tf_op jit(solution)/shard_map/reduce_scatter | solution.py:76
  570.9 0.7 copy-start.13
  570.9 1.4 copy-start.3
  570.9 2.1 copy-start.1
  571.0 77.4 %all-reduce.7.cloned.1.call-start = ((), (), s32[]{:S(2)}) async-start(), calls=%async_computation.23 | async-start | bytes 131072 | tf_op jit(solution)/shard_map/psum | solution.py:95
  573.1 34.2 %copy-start.5 = (bf16[6,1024,128]{2,1,0:T(8,128)(2,1)S(1)}, bf16[6,1024,128]{2,1,0:T(8,128)(2,1)}, u32[]{:S(2)}) copy-start(bf16[6,1024,128]{2,1,0:T(8,128)(2,1)} %param.48) | copy-start | bytes 4718596
  573.1 75.3 %copy-start.9 = (bf16[128,1024]{1,0:T(8,128)(2,1)S(1)}, bf16[128,1024]{1,0:T(8,128)(2,1)}, u32[]{:S(2)}) copy-start(bf16[128,1024]{1,0:T(8,128)(2,1)} %reduce-scatter.11.cloned.1.call-done) | copy-start | bytes 786436
  573.1 75.3 %copy-start.10 = (bf16[128,1024]{1,0:T(8,128)(2,1)S(1)}, bf16[128,1024]{1,0:T(8,128)(2,1)}, u32[]{:S(2)}) copy-start(bf16[128,1024]{1,0:T(8,128)(2,1)} %reduce-scatter.13.cloned.1.call-done) | copy-start | bytes 786436
  573.1 75.3 %copy-start.11 = (bf16[128,1024]{1,0:T(8,128)(2,1)S(1)}, bf16[128,1024]{1,0:T(8,128)(2,1)}, u32[]{:S(2)}) copy-start(bf16[128,1024]{1,0:T(8,128)(2,1)} %reduce-scatter.9.cloned.1.call-done) | copy-start | bytes 786436
  607.2 70.0 %all-gather.29.cloned.1.call-start = ((), (), s32[]{:S(2)}) async-start(), calls=%async_computation.31 | async-start | bytes 1310720 | tf_op jit(solution)/shard_map/all_gather | solution.py:74
  650.5 97.7 %reduce-scatter.19.cloned.1.call-start = ((), (), s32[]{:S(2)}) async-start(), calls=%async_computation.24 | async-start | bytes 2359296 | tf_op jit(solution)/shard_map/reduce_scatter | solution.py:76
  713.9 0.7 copy-start.12
  713.9 84.5 %all-gather.31.cloned.1.call-start = ((), (), s32[]{:S(2)}) async-start(), calls=%async_computation.32 | async-start | bytes 1310720 | tf_op jit(solution)/shard_map/all_gather | solution.py:74
  775.0 94.5 %reduce-scatter.21.cloned.1.call-start = ((), (), s32[]{:S(2)}) async-start(), calls=%async_computation.25 | async-start | bytes 2359296 | tf_op jit(solution)/shard_map/reduce_scatter | solution.py:76
  835.3 69.8 %all-gather.33.cloned.1.call-start = ((), (), s32[]{:S(2)}) async-start(), calls=%async_computation.33 | async-start | bytes 1310720 | tf_op jit(solution)/shard_map/all_gather | solution.py:74
  881.1 94.9 %reduce-scatter.23.cloned.1.call-start = ((), (), s32[]{:S(2)}) async-start(), calls=%async_computation.26 | async-start | bytes 2359296 | tf_op jit(solution)/shard_map/reduce_scatter | solution.py:76
  941.8 34.2 %copy-start.6 = (bf16[128,1024]{1,0:T(8,128)(2,1)S(1)}, bf16[128,1024]{1,0:T(8,128)(2,1)}, u32[]{:S(2)}) copy-start(bf16[128,1024]{1,0:T(8,128)(2,1)} %reduce-scatter.19.cloned.1.call-done) | copy-start | bytes 786436
  941.8 34.2 %copy-start.7 = (bf16[128,1024]{1,0:T(8,128)(2,1)S(1)}, bf16[128,1024]{1,0:T(8,128)(2,1)}, u32[]{:S(2)}) copy-start(bf16[128,1024]{1,0:T(8,128)(2,1)} %reduce-scatter.21.cloned.1.call-done) | copy-start | bytes 786436
  941.8 34.2 %copy-start.8 = (bf16[128,1024]{1,0:T(8,128)(2,1)S(1)}, bf16[128,1024]{1,0:T(8,128)(2,1)}, u32[]{:S(2)}) copy-start(bf16[128,1024]{1,0:T(8,128)(2,1)} %reduce-scatter.17.cloned.1.call-done) | copy-start | bytes 786436
Sparse Core Ops, SparseCore 0:
  9.2 29.2 all-gather.20
  74.1 34.0 reduce-scatter.8
  111.1 40.3 all-reduce.4
  154.3 26.4 all-gather.22
  217.7 34.0 reduce-scatter.10
  254.5 40.4 all-reduce.8
  297.0 26.4 all-gather.24
  360.4 34.0 reduce-scatter.12
  414.1 22.9 all-gather.26
  473.9 34.0 reduce-scatter.14
  509.8 24.9 all-gather.18
  571.1 34.0 reduce-scatter.16
  608.0 40.3 all-reduce.6
  650.7 26.4 all-gather.28
  714.1 34.1 reduce-scatter.18
  775.1 23.3 all-gather.30
  835.4 34.0 reduce-scatter.20
  881.2 23.8 all-gather.32
  941.9 34.0 reduce-scatter.22
